TPU v7x, 64 devices: a 2x2x8 block of a 4x4x8 slice. The times are simulated.
64 devices in a mesh: batch: 4 (over x, y), col: 16 (over z, core).
Axes of the slice: x: 2, y: 2, z: 8, core: 2. Of those that a mesh axis runs over, the one named last changes fastest.
The devices are a block of a 4x4x8 slice.
Arguments:
- lower: bfloat16 [16384, 4096], P('batch', 'col'), parts along dimension 0
- rhs: bfloat16 [16384, 16384], P('batch', 'col'), parts along dimension 0
Outputs:
- output: bfloat16 [16384, 16384], P('batch', 'col'), parts along dimension 0
There are 4 independent parts. A program takes and returns all parts, laid end to end along the dimension named above; each array names one.
All inputs are finite; a program needn't handle non-finite values.
Results may differ from a plain program's by a relative error of at most 0.001.
Values are sent between devices in bfloat16 or wider.
A program may use at most 768 MiB of HBM per device.

v0:
```python
import functools

import jax
import jax.numpy as jnp
from jax import lax
from jax.experimental import pallas as pl
from jax.experimental.pallas import tpu as pltpu
from jax.sharding import PartitionSpec as P

BLOCK = 256
MESH = pl.DeviceIdType.MESH
CHIPS = 8
PLUS_HOPS = (2, 2, 3, 5, 4, 4, 3, 2)
LONGER = {(0, 3): 12, (1, 3): 7, (1, 4): 13, (2, 4): 6, (2, 5): 8}
UP = 1
SPARE = 16
SLOTS = 36
RING = 19
LAPS = 8
LATER = (0, 3)


def pick(index, values):
    out = jnp.int32(values[-1])
    for j in range(len(values) - 2, -1, -1):
        out = jnp.where(index == j, jnp.int32(values[j]), out)
    return out


def kernel(nb, l_ref, b_ref, acc, lv, dg, raw, bv, isem, osem, fsem, dsem, bsem, credit):
    c = lax.axis_index("col")
    z, p = c // 2, c % 2
    q = 1 - p
    mate = z * 2 + q
    way = 1 - 2 * UP
    ahead = ((z + CHIPS + way * (1 - 2 * p)) % CHIPS) * 2 + p
    behind = ((z + CHIPS - way * (1 - 2 * p)) % CHIPS) * 2 + p
    half = BLOCK // 2
    first_slots = nb - 2 * z
    later = pick(p, LATER)

    def split(s, d):
        t = jnp.where(d <= pick(s, PLUS_HOPS), 0, nb)
        for (s0, d0), v in LONGER.items():
            t = jnp.where(s * CHIPS + d == s0 * CHIPS + d0, v, t)
        return t

    def bounds(core, d):
        s = (z + CHIPS - way * (1 - 2 * core) * d) % CHIPS
        plus = core == UP
        here = split(s, jnp.where(plus, d, CHIPS - d))
        on = split(s, jnp.where(plus, d + 1, CHIPS - 1 - d))
        low = jnp.where(plus, jnp.maximum(2 * s, here), 2 * s)
        high = jnp.where(plus, nb, here)
        on_low = jnp.where(plus, jnp.maximum(2 * s, on), 2 * s)
        on_high = jnp.where(plus, nb, on)
        return s, low, high, on_low, on_high

    def inside(i, low, high):
        return (i >= low) & (i < high)

    def start(core, d):
        _, low, high, _, _ = bounds(core, d)
        return jnp.where(low < high, jnp.where(core == UP, high - 1, low), -1)

    def advance(core, d, i):
        _, low, high, _, _ = bounds(core, d)
        j = jnp.where(core == UP, i - 1, i + 1)
        more = inside(j, low, high)
        ended = i < 0
        j = jnp.where(more, j, start(core, d + 1))
        return jnp.where(more | ended, d, d + 1), jnp.where(ended, i, j)

    def look(core, d, i):
        s, low, high, on_low, on_high = bounds(core, d)
        return s, inside(i, low, high), inside(i, on_low, on_high)

    def place(s, i):
        return (nb - 1) * s - s * (s - 1) + i - 2 * s - 1

    def each(k, i, fn):
        @pl.when(i == k)
        def _():
            fn(dg.at[k])

        @pl.when(i != k)
        def _():
            fn(lv.at[place(k // 2, i), k % 2])

    def strip(s, i, fn, whole):
        @pl.when(i == 2 * s)
        def _():
            fn(dg.at[i])

        @pl.when(i == 2 * s + 1)
        def _():
            if whole:
                fn(bv.at[pl.ds(0, 3 * BLOCK + SPARE), pl.ds(0, half)])
            else:
                fn(lv.at[place(s, i), 0])
                fn(dg.at[i])

        @pl.when(i > 2 * s + 1)
        def _():
            fn(lv.at[place(s, i)])

    def remote(ref, out, arrive, dev):
        return pltpu.make_async_remote_copy(
            src_ref=ref, dst_ref=ref, send_sem=out, recv_sem=arrive,
            device_id={"col": dev}, device_id_type=MESH)

    def send(s, i, out, arrive, dev):
        strip(s, i, lambda ref: remote(ref, out, arrive, dev).start(), False)

    def sent(s, i, out, dev):
        strip(s, i, lambda ref: remote(ref, out, isem.at[0], dev).wait_send(), True)

    def land(s, i, arrive):
        strip(s, i, lambda ref: remote(ref, fsem.at[0], arrive, ahead).wait_recv(), True)

    def out_sem(m):
        return fsem.at[m % RING]

    barrier = pltpu.get_barrier_semaphore()
    for dev in (behind, mate):
        pl.semaphore_signal(barrier, inc=1, device_id={"col": dev}, device_id_type=MESH)

    diag_row = pl.multiple_of(c * BLOCK, BLOCK)
    quarter = [
        pltpu.make_async_copy(l_ref.at[pl.ds(diag_row, half), pl.ds(0, half)], raw.at[0], fsem.at[0]),
        pltpu.make_async_copy(l_ref.at[pl.ds(diag_row + half, half), pl.ds(half, half)], raw.at[1], fsem.at[1]),
        pltpu.make_async_copy(
            l_ref.at[pl.ds(diag_row + half, half), pl.ds(0, half)], dg.at[c, pl.ds(half, half), :], fsem.at[2]),
    ]
    for copy in quarter:
        copy.start()
    row = lax.broadcasted_iota(jnp.int32, (half, half), 0)
    col = lax.broadcasted_iota(jnp.int32, (half, half), 1)

    def own_copy(i):
        rows = pl.ds(pl.multiple_of(i * BLOCK, BLOCK), BLOCK)
        return pltpu.make_async_copy(l_ref.at[rows, :], lv.at[place(z, i), p], dsem.at[i])

    def b_copy(k):
        rows = pl.ds(pl.multiple_of(k * BLOCK, BLOCK), BLOCK)
        return pltpu.make_async_copy(b_ref.at[rows, :], bv.at[rows, :], bsem)

    lax.fori_loop(c + 1, nb, lambda i, x: (own_copy(i).start(), x)[1], 0)
    for copy in quarter:
        copy.wait()
    corner = raw[1].astype(jnp.float32)
    dg[c, :half, :] = jnp.where(row >= col, raw[0].astype(jnp.float32), corner.T).astype(dg.dtype)
    line = jnp.sum(jnp.where(row == col, corner, 0.0), axis=0, keepdims=True)
    dg[c, BLOCK:, :] = jnp.broadcast_to(line, (SPARE, half)).astype(dg.dtype)
    lax.fori_loop(c + 1, nb, lambda i, x: (own_copy(i).wait(), x)[1], 0)
    lax.fori_loop(0, nb, lambda k, x: (b_copy(k).start(), x)[1], 0)
    pl.semaphore_wait(barrier, 2)

    def send_tile(k, i, out, arrive, dev):
        each(k, i, lambda ref: remote(ref, out, arrive, dev).start())

    head = jnp.where(p == UP, 0, p)
    send_tile(c, jnp.where(p == UP, nb - 1, c), out_sem(head), isem.at[head], ahead)

    def to_mate(j, carry):
        i = jnp.where(p == UP, c + j, nb - 1 - j)
        send_tile(c, i, dsem.at[i], osem.at[i], mate)
        return carry

    lax.fori_loop(0, nb - c, to_mate, 0)

    def send_first(j, carry):
        i = jnp.where(p == UP, nb - 1 - j, 2 * z + j)

        @pl.when((i >= c) & (j != head))
        def _():
            send_tile(c, i, out_sem(j), isem.at[j], ahead)

        @pl.when(i >= mate)
        def _():
            each(mate, i, lambda ref: remote(ref, fsem.at[0], osem.at[i], ahead).wait_recv())
            send_tile(mate, i, out_sem(j), isem.at[j], ahead)

        return carry

    lax.fori_loop(0, first_slots, send_first, 0)
    pl.semaphore_signal(credit, inc=LAPS, device_id={"col": mate}, device_id_type=MESH)

    def mate_has(i, carry):
        each(c, i, lambda ref: remote(ref, dsem.at[i], isem.at[0], mate).wait_send())
        return carry

    lax.fori_loop(c, nb, mate_has, 0)

    def clear(i, carry):
        acc[pl.ds(pl.multiple_of(i * 64, 64), 64), :] = jnp.zeros((64, acc.shape[1]), jnp.float32)
        return carry

    lax.fori_loop(0, acc.shape[0] // 64, clear, 0)
    pltpu.make_async_copy(b_ref, bv, bsem).wait()

    width = acc.shape[1] // 2
    parts = [slice(n * width, (n + 1) * width) for n in range(2)]

    def use(s, i):
        at = pl.multiple_of(i * BLOCK, BLOCK)
        depth = pl.multiple_of(2 * s * BLOCK, BLOCK)

        @pl.when(i > 2 * s + 1)
        def _():
            left, right = lv[place(s, i), 0], lv[place(s, i), 1]
            for cols in parts:
                acc[pl.ds(at, BLOCK), cols] += jnp.dot(
                    left, bv[pl.ds(depth, BLOCK), cols], preferred_element_type=jnp.float32) + jnp.dot(
                    right, bv[pl.ds(depth + BLOCK, BLOCK), cols], preferred_element_type=jnp.float32)

        @pl.when(i == 2 * s + 1)
        def _():
            left = lv[place(s, i), 0]
            for cols in parts:
                acc[pl.ds(at, BLOCK), cols] += jnp.dot(
                    left, bv[pl.ds(depth, BLOCK), cols], preferred_element_type=jnp.float32)

        @pl.when(i <= 2 * s + 1)
        def _():
            both = dg[i, :half, :].astype(jnp.float32)
            line = dg[i, BLOCK:BLOCK + 1, :].astype(jnp.float32)
            top = jnp.where(row >= col, both, 0.0).astype(lv.dtype)
            left = dg[i, half:BLOCK, :]
            corner = jnp.where(row < col, both, jnp.where(row == col, line, 0.0)).T.astype(lv.dtype)
            for cols in parts:
                upper = bv[pl.ds(at, half), cols]
                lower = bv[pl.ds(at + half, half), cols]
                acc[pl.ds(at, half), cols] += jnp.dot(top, upper, preferred_element_type=jnp.float32)
                acc[pl.ds(at + half, half), cols] += jnp.dot(
                    left, upper, preferred_element_type=jnp.float32) + jnp.dot(
                    corner, lower, preferred_element_type=jnp.float32)

    def left_onward(m, d, i):
        s, _, on = look(p, d, i)

        @pl.when(on)
        def _():
            sent(s, i, out_sem(m), ahead)

        return advance(p, d, i)

    def step(n, cur):
        d, i, qd, qi, od, oi, gone = cur
        s, here, on = look(p, d, i)
        pl.semaphore_wait(credit, 1)

        @pl.when(here)
        def _():
            land(s, i, isem.at[n])

            @pl.when(on)
            def _():
                send(s, i, out_sem(first_slots + n), isem.at[gone], ahead)

            send(s, i, dsem.at[0], osem.at[n % LAPS], mate)

        late = n >= later
        qs, there, _ = look(q, qd, jnp.where(late, qi, -1))
        lap_in = (n + LAPS - later) % LAPS
        at_home = 2 * z + n
        groups = ((s, i, here), (z, at_home, at_home < nb), (qs, qi, there))

        def one(j, carry):
            k, r, v = (
                jnp.where(j == 0, x, jnp.where(j == 1, y, w))
                for x, y, w in zip(*[(g[0], g[1], g[2].astype(jnp.int32)) for g in groups]))

            @pl.when(v > 0)
            def _():
                @pl.when(j == 2)
                def _():
                    land(k, r, osem.at[lap_in])

                use(k, r)

            return carry

        lax.fori_loop(0, 3, one, 0)

        @pl.when(late & (n - later < SLOTS - LAPS))
        def _():
            pl.semaphore_signal(credit, inc=1, device_id={"col": mate}, device_id_type=MESH)

        @pl.when(here)
        def _():
            sent(s, i, dsem.at[0], mate)

        again = n >= 2
        e, f = left_onward(jnp.maximum(n - 2, 0), od, jnp.where(again, oi, -1))
        g, h = advance(q, qd, qi)
        return (*advance(p, d, i), jnp.where(late, g, qd), jnp.where(late, h, qi),
                jnp.where(again, e, od), jnp.where(again, f, oi), gone + on.astype(jnp.int32))

    zero, one_ = jnp.int32(0), jnp.int32(1)
    state = lax.fori_loop(0, SLOTS, step, (
        one_, start(p, one_), one_, start(q, one_), zero, start(p, zero), first_slots))
    qd, qi, od, oi = state[2:6]
    left = zero
    for more in range(2):
        _, _, _, on_low, on_high = bounds(p, od + more)
        left = jnp.where((oi >= 0) & (on_low < on_high), first_slots + 2, left)
    lax.fori_loop(0, left, lambda m, cur: left_onward(SLOTS - 2 + m, *cur), (od, oi))

    def drain(m, cur):
        qd, qi = cur
        s, there, _ = look(q, qd, qi)

        @pl.when(there)
        def _():
            land(s, qi, osem.at[m % LAPS])
            use(s, qi)

        return advance(q, qd, qi)

    lax.fori_loop(SLOTS - later, SLOTS, drain, (qd, qi))


def round_kernel(x_ref, o_ref, buf, sem):
    chunks, step = 16, 64
    rows = x_ref.shape[0] // chunks
    step = min(step, rows)

    def one(j, carry):
        def some(m, carry):
            part = pl.ds(pl.multiple_of(j * rows + m * step, step), step)
            buf[part, :] = x_ref[part, :].astype(buf.dtype)
            return carry

        lax.fori_loop(0, rows // step, some, 0)
        part = pl.ds(pl.multiple_of(j * rows, rows), rows)
        pltpu.make_async_copy(buf.at[part, :], o_ref.at[part, :], sem).start()
        return carry

    lax.fori_loop(0, chunks, one, 0)
    pltpu.make_async_copy(buf, o_ref, sem).wait()


def solution(mesh):
    def local(l_cols, b_cols):
        order, width = b_cols.shape
        nb = order // BLOCK
        strips = sum(nb - 1 - 2 * s for s in range(nb // 2))
        l_cols = pltpu.with_memory_space_constraint(l_cols, pltpu.HBM)
        b_cols = pltpu.with_memory_space_constraint(b_cols, pltpu.HBM)
        acc = pl.pallas_call(
            functools.partial(kernel, nb),
            out_shape=pltpu.VMEM((order, width), jnp.float32),
            in_specs=[pl.BlockSpec(memory_space=pltpu.HBM)] * 2,
            out_specs=pl.BlockSpec(memory_space=pltpu.VMEM),
            scratch_shapes=[
                pltpu.VMEM((strips, 2, BLOCK, BLOCK), jnp.bfloat16),
                pltpu.VMEM((nb, BLOCK + SPARE, BLOCK // 2), jnp.bfloat16),
                pltpu.VMEM((2, BLOCK // 2, BLOCK // 2), jnp.bfloat16),
                pltpu.VMEM((order, width), jnp.bfloat16),
                pltpu.SemaphoreType.DMA((SLOTS,)),
                pltpu.SemaphoreType.DMA((max(nb, LAPS),)),
                pltpu.SemaphoreType.DMA((RING,)),
                pltpu.SemaphoreType.DMA((nb,)),
                pltpu.SemaphoreType.DMA,
                pltpu.SemaphoreType.REGULAR,
            ],
            compiler_params=pltpu.CompilerParams(
                collective_id=0, has_side_effects=True, vmem_limit_bytes=34 * 2**20),
        )(l_cols, b_cols)
        return pl.pallas_call(
            round_kernel,
            out_shape=jax.ShapeDtypeStruct((order, width), jnp.bfloat16),
            in_specs=[pl.BlockSpec(memory_space=pltpu.VMEM)],
            out_specs=pl.BlockSpec(memory_space=pltpu.HBM),
            scratch_shapes=[
                pltpu.VMEM((order, width), jnp.bfloat16),
                pltpu.SemaphoreType.DMA,
            ],
            compiler_params=pltpu.CompilerParams(vmem_limit_bytes=16 * 2**20),
        )(acc)

    return jax.shard_map(local, mesh=mesh, in_specs=(P("batch", "col"), P("batch", "col")),
                         out_specs=P("batch", "col"), check_vma=False)
```

profile of v0, /device:TPU:22, one launch (start us, length us, event | category | flops | bytes accessed | tf_op | source)
XLA Modules:
  0.0 99.8 jit_solution(14341623523880875400)
XLA Ops:
  0.0 96.5 %shard_map.28.x_ref = f32[4096,1024]{1,0:T(8,128)S(1)} custom-call(bf16[4096,256]{1,0:T(8,128)(2,1)} %l_ref.1, bf16[4096,1024]{1,0:T(8,128)(2,1)} %b_ref.1), custom_call_target="tpu_custom_call" | custom-call | tf_op jit(solution)/shard_map/pallas_call | solution.py:351
  96.5 3.3 %shard_map.29 = bf16[4096,1024]{1,0:T(8,128)(2,1)} custom-call(f32[4096,1024]{1,0:T(8,128)S(1)} %shard_map.28.x_ref), custom_call_target="tpu_custom_call" | custom-call | tf_op jit(solution)/shard_map/pallas_call | solution.py:371
where the time goes:
time: 100 us; the launch traced here: 99.8 us
  Pallas kernels  99.8 us (100%)
    pallas_call x1, Pallas kernels, local(): pl.pallas_call(functools.partial(kernel, nb), out_shape=pltpu.VMEM((order...  96.5 us
    pallas_call x1, Pallas kernels, local(): pl.pallas_call(round_kernel, out_shape=jax.ShapeDtypeStruct((order, width...  3.35 us

commit v1 on v0

--- a/solution.py
+++ b/solution.py
@@ -11,13 +11,14 @@
 MESH = pl.DeviceIdType.MESH
 CHIPS = 8
 PLUS_HOPS = (2, 2, 3, 5, 4, 4, 3, 2)
-LONGER = {(0, 3): 12, (1, 3): 7, (1, 4): 13, (2, 4): 6, (2, 5): 8}
+LONGER = {(0, 3): 12, (1, 3): 7, (1, 4): 13, (2, 4): 5, (2, 5): 7}
+LATE_FIRST = (2, 7)
 UP = 1
 SPARE = 16
-SLOTS = 36
+SLOTS = 37
 RING = 19
 LAPS = 8
-LATER = (0, 3)
+LATER = (-1, 3)
 
 
 def pick(index, values):
@@ -71,9 +72,14 @@
         j = jnp.where(more, j, start(core, d + 1))
         return jnp.where(more | ended, d, d + 1), jnp.where(ended, i, j)
 
-    def look(core, d, i):
+    def strip_at(s, r):
+        s0, last = LATE_FIRST
+        moved = jnp.where(r < last, r + 1, 2 * s0)
+        return jnp.where((s == s0) & inside(r, 2 * s0, last + 1), moved, r)
+
+    def look(core, d, r):
         s, low, high, on_low, on_high = bounds(core, d)
-        return s, inside(i, low, high), inside(i, on_low, on_high)
+        return s, strip_at(s, r), inside(r, low, high), inside(r, on_low, on_high)
 
     def place(s, i):
         return (nb - 1) * s - s * (s - 1) + i - 2 * s - 1
@@ -160,7 +166,7 @@
         each(k, i, lambda ref: remote(ref, out, arrive, dev).start())
 
     head = jnp.where(p == UP, 0, p)
-    send_tile(c, jnp.where(p == UP, nb - 1, c), out_sem(head), isem.at[head], ahead)
+    send_tile(c, jnp.where(p == UP, nb - 1, strip_at(z, 2 * z + head)), out_sem(head), isem.at[head], ahead)
 
     def to_mate(j, carry):
         i = jnp.where(p == UP, c + j, nb - 1 - j)
@@ -170,7 +176,7 @@
     lax.fori_loop(0, nb - c, to_mate, 0)
 
     def send_first(j, carry):
-        i = jnp.where(p == UP, nb - 1 - j, 2 * z + j)
+        i = strip_at(z, jnp.where(p == UP, nb - 1 - j, 2 * z + j))
 
         @pl.when((i >= c) & (j != head))
         def _():
@@ -237,37 +243,37 @@
                     corner, lower, preferred_element_type=jnp.float32)
 
     def left_onward(m, d, i):
-        s, _, on = look(p, d, i)
+        s, r, _, on = look(p, d, i)
 
         @pl.when(on)
         def _():
-            sent(s, i, out_sem(m), ahead)
+            sent(s, r, out_sem(m), ahead)
 
         return advance(p, d, i)
 
     def step(n, cur):
         d, i, qd, qi, od, oi, gone = cur
-        s, here, on = look(p, d, i)
+        s, r, here, on = look(p, d, i)
         pl.semaphore_wait(credit, 1)
 
         @pl.when(here)
         def _():
-            land(s, i, isem.at[n])
+            land(s, r, isem.at[n])
 
             @pl.when(on)
             def _():
-                send(s, i, out_sem(first_slots + n), isem.at[gone], ahead)
-
-            send(s, i, dsem.at[0], osem.at[n % LAPS], mate)
+                send(s, r, out_sem(first_slots + n), isem.at[gone], ahead)
+
+            send(s, r, dsem.at[0], osem.at[n % LAPS], mate)
 
         late = n >= later
-        qs, there, _ = look(q, qd, jnp.where(late, qi, -1))
+        qs, qr, there, _ = look(q, qd, jnp.where(late, qi, -1))
         lap_in = (n + LAPS - later) % LAPS
         at_home = 2 * z + n
-        groups = ((s, i, here), (z, at_home, at_home < nb), (qs, qi, there))
+        groups = ((s, r, here), (z, at_home, at_home < nb), (qs, qr, there))
 
         def one(j, carry):
-            k, r, v = (
+            k, h, v = (
                 jnp.where(j == 0, x, jnp.where(j == 1, y, w))
                 for x, y, w in zip(*[(g[0], g[1], g[2].astype(jnp.int32)) for g in groups]))
 
@@ -275,9 +281,9 @@
             def _():
                 @pl.when(j == 2)
                 def _():
-                    land(k, r, osem.at[lap_in])
-
-                use(k, r)
+                    land(k, h, osem.at[lap_in])
+
+                use(k, h)
 
             return carry
 
@@ -289,34 +295,39 @@
 
         @pl.when(here)
         def _():
-            sent(s, i, dsem.at[0], mate)
+            sent(s, r, dsem.at[0], mate)
 
         again = n >= 2
         e, f = left_onward(jnp.maximum(n - 2, 0), od, jnp.where(again, oi, -1))
-        g, h = advance(q, qd, qi)
-        return (*advance(p, d, i), jnp.where(late, g, qd), jnp.where(late, h, qi),
+        g, e2 = advance(q, qd, qi)
+        return (*advance(p, d, i), jnp.where(late, g, qd), jnp.where(late, e2, qi),
                 jnp.where(again, e, od), jnp.where(again, f, oi), gone + on.astype(jnp.int32))
 
+    def drain(m, cur):
+        qd, qi = cur
+        s, r, there, _ = look(q, qd, qi)
+
+        @pl.when(there)
+        def _():
+            land(s, r, osem.at[m % LAPS])
+            use(s, r)
+
+        @pl.when(m < SLOTS - LAPS)
+        def _():
+            pl.semaphore_signal(credit, inc=1, device_id={"col": mate}, device_id_type=MESH)
+
+        return advance(q, qd, qi)
+
     zero, one_ = jnp.int32(0), jnp.int32(1)
+    qd, qi = lax.fori_loop(0, jnp.maximum(-later, 0), drain, (one_, start(q, one_)))
     state = lax.fori_loop(0, SLOTS, step, (
-        one_, start(p, one_), one_, start(q, one_), zero, start(p, zero), first_slots))
+        one_, start(p, one_), qd, qi, zero, start(p, zero), first_slots))
     qd, qi, od, oi = state[2:6]
     left = zero
     for more in range(2):
         _, _, _, on_low, on_high = bounds(p, od + more)
         left = jnp.where((oi >= 0) & (on_low < on_high), first_slots + 2, left)
     lax.fori_loop(0, left, lambda m, cur: left_onward(SLOTS - 2 + m, *cur), (od, oi))
-
-    def drain(m, cur):
-        qd, qi = cur
-        s, there, _ = look(q, qd, qi)
-
-        @pl.when(there)
-        def _():
-            land(s, qi, osem.at[m % LAPS])
-            use(s, qi)
-
-        return advance(q, qd, qi)
 
     lax.fori_loop(SLOTS - later, SLOTS, drain, (qd, qi))
 

time: 100 us -> 101 us (1.010); the launches traced: 99.8 us -> 99.1 us
  no operation moved by 1% of the time
where the time goes in v1:
time: 101 us; the launch traced here: 99.1 us
  Pallas kernels  99.1 us (98%)
    pallas_call x1, Pallas kernels, local(): pl.pallas_call(functools.partial(kernel, nb), out_shape=pltpu.VMEM((order...  95.7 us
    pallas_call x1, Pallas kernels, local(): pl.pallas_call(round_kernel, out_shape=jax.ShapeDtypeStruct((order, width...  3.35 us

profile of v1, /device:TPU:22, one launch (start us, length us, event | category | flops | bytes accessed | tf_op | source)
XLA Modules:
  0.0 99.1 jit_solution(7589045918646599132)
XLA Ops:
  0.0 95.7 %shard_map.28.x_ref = f32[4096,1024]{1,0:T(8,128)S(1)} custom-call(bf16[4096,256]{1,0:T(8,128)(2,1)} %l_ref.1, bf16[4096,1024]{1,0:T(8,128)(2,1)} %b_ref.1), custom_call_target="tpu_custom_call" | custom-call | tf_op jit(solution)/shard_map/pallas_call | solution.py:362
  95.8 3.3 %shard_map.29 = bf16[4096,1024]{1,0:T(8,128)(2,1)} custom-call(f32[4096,1024]{1,0:T(8,128)S(1)} %shard_map.28.x_ref), custom_call_target="tpu_custom_call" | custom-call | tf_op jit(solution)/shard_map/pallas_call | solution.py:382

commit v2 on v1

--- a/solution.py
+++ b/solution.py
@@ -11,7 +11,7 @@
 MESH = pl.DeviceIdType.MESH
 CHIPS = 8
 PLUS_HOPS = (2, 2, 3, 5, 4, 4, 3, 2)
-LONGER = {(0, 3): 12, (1, 3): 7, (1, 4): 13, (2, 4): 5, (2, 5): 7}
+LONGER = {(0, 3): 12, (1, 3): 7, (1, 4): 13, (2, 4): 6, (2, 5): 7}
 LATE_FIRST = (2, 7)
 UP = 1
 SPARE = 16

time: 101 us -> 103 us (1.020)
  the two profiles are of different devices: /device:TPU:22 before, /device:TPU:215 now
where the time goes in v2:
time: 103 us
  Pallas kernels  103 us (100%)
    pallas_call x1, Pallas kernels, local(): pl.pallas_call(functools.partial(kernel, nb), out_shape=pltpu.VMEM((order...  99.9 us
    pallas_call x1, Pallas kernels, local(): pl.pallas_call(round_kernel, out_shape=jax.ShapeDtypeStruct((order, width...  3.35 us

profile of v2, /device:TPU:215, one launch (start us, length us, event | category | flops | bytes accessed | tf_op | source)
XLA Modules:
  0.0 103.2 jit_solution(11684292427162254396)
XLA Ops:
  0.0 99.9 %shard_map.28.x_ref = f32[4096,1024]{1,0:T(8,128)S(1)} custom-call(bf16[4096,256]{1,0:T(8,128)(2,1)} %l_ref.1, bf16[4096,1024]{1,0:T(8,128)(2,1)} %b_ref.1), custom_call_target="tpu_custom_call" | custom-call | tf_op jit(solution)/shard_map/pallas_call | solution.py:362
  99.9 3.3 %shard_map.29 = bf16[4096,1024]{1,0:T(8,128)(2,1)} custom-call(f32[4096,1024]{1,0:T(8,128)S(1)} %shard_map.28.x_ref), custom_call_target="tpu_custom_call" | custom-call | tf_op jit(solution)/shard_map/pallas_call | solution.py:382

commit v3 on v0

--- a/solution.py
+++ b/solution.py
@@ -9,7 +9,6 @@
 
 BLOCK = 256
 MESH = pl.DeviceIdType.MESH
-CHIPS = 8
 PLUS_HOPS = (2, 2, 3, 5, 4, 4, 3, 2)
 LONGER = {(0, 3): 12, (1, 3): 7, (1, 4): 13, (2, 4): 6, (2, 5): 8}
 UP = 1
@@ -27,14 +26,14 @@
     return out
 
 
-def kernel(nb, l_ref, b_ref, acc, lv, dg, raw, bv, isem, osem, fsem, dsem, bsem, credit):
+def kernel(nb, chips, l_ref, b_ref, acc, lv, dg, raw, bv, isem, osem, fsem, dsem, bsem, credit):
     c = lax.axis_index("col")
     z, p = c // 2, c % 2
     q = 1 - p
     mate = z * 2 + q
     way = 1 - 2 * UP
-    ahead = ((z + CHIPS + way * (1 - 2 * p)) % CHIPS) * 2 + p
-    behind = ((z + CHIPS - way * (1 - 2 * p)) % CHIPS) * 2 + p
+    ahead = ((z + chips + way * (1 - 2 * p)) % chips) * 2 + p
+    behind = ((z + chips - way * (1 - 2 * p)) % chips) * 2 + p
     half = BLOCK // 2
     first_slots = nb - 2 * z
     later = pick(p, LATER)
@@ -42,14 +41,14 @@
     def split(s, d):
         t = jnp.where(d <= pick(s, PLUS_HOPS), 0, nb)
         for (s0, d0), v in LONGER.items():
-            t = jnp.where(s * CHIPS + d == s0 * CHIPS + d0, v, t)
+            t = jnp.where(s * chips + d == s0 * chips + d0, v, t)
         return t
 
     def bounds(core, d):
-        s = (z + CHIPS - way * (1 - 2 * core) * d) % CHIPS
+        s = (z + chips - way * (1 - 2 * core) * d) % chips
         plus = core == UP
-        here = split(s, jnp.where(plus, d, CHIPS - d))
-        on = split(s, jnp.where(plus, d + 1, CHIPS - 1 - d))
+        here = split(s, jnp.where(plus, d, chips - d))
+        on = split(s, jnp.where(plus, d + 1, chips - 1 - d))
         low = jnp.where(plus, jnp.maximum(2 * s, here), 2 * s)
         high = jnp.where(plus, nb, here)
         on_low = jnp.where(plus, jnp.maximum(2 * s, on), 2 * s)
@@ -342,6 +341,8 @@
 
 
 def solution(mesh):
+    chips = mesh.shape["col"] // 2
+
     def local(l_cols, b_cols):
         order, width = b_cols.shape
         nb = order // BLOCK
@@ -349,7 +350,7 @@
         l_cols = pltpu.with_memory_space_constraint(l_cols, pltpu.HBM)
         b_cols = pltpu.with_memory_space_constraint(b_cols, pltpu.HBM)
         acc = pl.pallas_call(
-            functools.partial(kernel, nb),
+            functools.partial(kernel, nb, chips),
             out_shape=pltpu.VMEM((order, width), jnp.float32),
             in_specs=[pl.BlockSpec(memory_space=pltpu.HBM)] * 2,
             out_specs=pl.BlockSpec(memory_space=pltpu.VMEM),

time: 100 us -> 100 us (level)
  no operation moved by 1% of the time
where the time goes in v3:
time: 100 us; the launch traced here: 99.8 us
  Pallas kernels  99.8 us (100%)
    pallas_call x1, Pallas kernels, local(): pl.pallas_call(functools.partial(kernel, nb, chips), out_shape=pltpu.VMEM...  96.5 us
    pallas_call x1, Pallas kernels, local(): pl.pallas_call(round_kernel, out_shape=jax.ShapeDtypeStruct((order, width...  3.35 us

profile of v3, /device:TPU:22, one launch (start us, length us, event | category | flops | bytes accessed | tf_op | source)
XLA Modules:
  0.0 99.8 jit_solution(14341623523880875400)
XLA Ops:
  0.0 96.5 %shard_map.28.x_ref = f32[4096,1024]{1,0:T(8,128)S(1)} custom-call(bf16[4096,256]{1,0:T(8,128)(2,1)} %l_ref.1, bf16[4096,1024]{1,0:T(8,128)(2,1)} %b_ref.1), custom_call_target="tpu_custom_call" | custom-call | tf_op jit(solution)/shard_map/pallas_call | solution.py:352
  96.5 3.3 %shard_map.29 = bf16[4096,1024]{1,0:T(8,128)(2,1)} custom-call(f32[4096,1024]{1,0:T(8,128)S(1)} %shard_map.28.x_ref), custom_call_target="tpu_custom_call" | custom-call | tf_op jit(solution)/shard_map/pallas_call | solution.py:372
